TPU v7x, 32 devices: a whole 2x2x4 slice. The times are simulated.
32 devices in a mesh: gx: 2 (over x), gy: 4 (over z), ta: 4 (over y, core).
Axes of the slice: x: 2, y: 2, z: 4, core: 2. Of those that a mesh axis runs over, the one named last changes fastest.
Arguments:
- traces: bfloat16 [131072, 1024], P(('gx', 'gy'), 'ta'), may hold values from -6 to 6
- interp: bfloat16 [2, 16], replicated, may hold values from -1.5 to 1.5
- translations: bfloat16 [4, 2048, 1024], P(None, ('gx', 'gy')), may hold values from -0.125 to 0.125
- leaf_slot: int32 [8192], P(('gx', 'gy', 'ta')), may hold values from 0 to 255, as said below
- pairing: int32 [4, 8192], P(None, ('gx', 'gy', 'ta')), may hold values from 0 to 255, as said below
Outputs:
- coefficients: bfloat16 [8192, 1024], P(('gx', 'gy', 'ta'))
Inputs may be any that keep to these rules, and one draw needn't show every extreme that they name: `leaf_slot`: each aligned block of 256 entries (the leaves of one device) is a permutation of 0 to 255. `pairing`: for every level, each aligned block of 256 entries along the leaves is a permutation of 0 to 255.
All inputs are finite; a program needn't handle non-finite values.
Results may differ from a plain program's by a relative error of at most 0.0082.
Values may be sent and summed in bfloat16 or wider, within the bound.
A program may use at most 128 MiB of HBM per device.

v0:
```python
import math

import jax
import jax.numpy as jnp
from jax import lax
from jax.sharding import PartitionSpec as P

NF = 256
CHEB = 2
BOXT = 16


def from_partner(value, axis, bit):
    mask = 2**bit
    pairs = [(source, source ^ mask) for source in range(lax.axis_size(axis))]
    return lax.ppermute(value, axis, pairs)


def spectrum_table(length, count):
    sample_pos = lax.broadcasted_iota(jnp.float32, (length, count), 0)
    frequency = lax.broadcasted_iota(jnp.float32, (length, count), 1) + 1.0
    angles = 2.0 * math.pi / length * jnp.mod(sample_pos * frequency, float(length))
    factor = math.sqrt(2.0 / length)
    return jnp.concatenate([jnp.cos(angles) * factor, -jnp.sin(angles) * factor], axis=1).astype(
        jnp.bfloat16
    )


def move_boxes(blocks):
    return lax.all_to_all(blocks, ("gx", "gy"), split_axis=0, concat_axis=0, tiled=True)


def on_device(traces, interp, translations, leaf_slot, pairing):
    regrouped = lax.all_to_all(traces, "ta", split_axis=0, concat_axis=1, tiled=True)
    sample_count = regrouped.shape[1]
    box_count = regrouped.shape[0] // BOXT
    sampled = jnp.einsum(
        "cb,kbt->kct",
        interp,
        regrouped.reshape(box_count, BOXT, sample_count),
        preferred_element_type=jnp.float32,
    )
    sampled = sampled.astype(jnp.bfloat16).reshape(box_count * CHEB, sample_count)
    fourier = spectrum_table(sample_count, NF)
    spectra = jnp.dot(sampled, fourier, preferred_element_type=jnp.float32)
    cheb_points = spectra.astype(jnp.bfloat16).reshape(box_count, CHEB * 2 * NF)
    arrived = move_boxes(cheb_points)
    states = jnp.take(arrived, leaf_slot, axis=0)
    log_devices = lax.axis_size(("gx", "gy", "ta")).bit_length() - 1
    level_count = translations.shape[0]
    every_level = lax.all_gather(translations, ("gx", "gy"), axis=1, tiled=True)
    for layer_index in range(level_count):
        flip_bit = layer_index * log_devices // level_count
        partner = from_partner(states, ("gx", "gy", "ta"), flip_bit)
        aligned = jnp.take(partner, pairing[layer_index], axis=0)
        joined = jnp.concatenate([states, aligned], axis=1)
        product_sum = jnp.dot(joined, every_level[layer_index], preferred_element_type=jnp.float32)
        states = product_sum.astype(jnp.bfloat16)
    return states


def solution(mesh):
    in_specs = (
        P(("gx", "gy"), "ta"),
        P(),
        P(None, ("gx", "gy"), None),
        P(("gx", "gy", "ta")),
        P(None, ("gx", "gy", "ta")),
    )
    out_specs = P(("gx", "gy", "ta"), None)
    return jax.shard_map(
        on_device, mesh=mesh, in_specs=in_specs, out_specs=out_specs, check_vma=False
    )
```

profile of v0, /device:TPU:0, one launch (start us, length us, event | category | flops | bytes accessed | tf_op | source)
XLA Modules:
  0.0 324.2 jit_solution(3128934555717147595)
XLA Ops:
  6.5 0.7 all-gather.2.cloned.1.call-update
  7.3 5.7 %all-to-all-start = ((bf16[4,4096,256]{2,1,0:T(8,128)(2,1)}), bf16[4,4096,256]{2,1,0:T(8,128)(2,1)}, u32[]{:S(2)}, u32[]{:S(2)}) async-start(bf16[4,4096,256]{2,1,0:T(8,128)(2,1)} %bitcast.35), calls=%async_computation | async-start | bytes 16777216 | tf_op jit(solution)/shard_map/all_to_all | solution.py:34
  13.0 4.8 %multiply_convert_fusion.1 = (bf16[1024,256]{1,0:T(8,128)(2,1)S(1)}, bf16[1024,256]{1,0:T(8,128)(2,1)S(1)}) fusion(f32[256]{0:T(256)S(1)} %iota_add_fusion), kind=kLoop, calls=%fused_computation.38 | loop fusion | flops 3407872 | bytes 1049600 | tf_op jit(solution)/shard_map/convert
  17.7 89.0 %all-to-all-done = bf16[4,4096,256]{2,1,0:T(8,128)(2,1)} async-done(((bf16[4,4096,256]{2,1,0:T(8,128)(2,1)}), bf16[4,4096,256]{2,1,0:T(8,128)(2,1)}, u32[]{:S(2)}, u32[]{:S(2)}) %all-to-all-start) | async-done | bytes 8388640 | tf_op jit(solution)/shard_map/all_to_all | solution.py:34
  106.7 12.2 %copy.7 = bf16[4096,4,256]{2,1,0:T(4,128)(2,1)} copy(bf16[4096,4,256]{2,0,1:T(8,128)(2,1)} %bitcast.1) | data formatting | bytes 16777216 | tf_op jit(solution)/shard_map/all_to_all | solution.py:34
  118.9 14.4 %reshape.19 = bf16[256,16,1024]{2,1,0:T(8,128)(2,1)} reshape(bf16[4096,4,256]{2,1,0:T(4,128)(2,1)} %copy.7) | data formatting | bytes 16777216 | tf_op jit(solution)/shard_map/reshape | solution.py:40
  133.3 5.6 %fusion.4 = bf16[256,2,1024]{2,1,0:T(2,128)(2,1)S(1)} fusion(bf16[256,16,1024]{2,1,0:T(8,128)(2,1)} %reshape.19, bf16[2,16]{1,0:T(2,128)(2,1)S(1)} %copy-done), kind=kOutput, calls=%fused_computation.15 | convolution fusion | flops 17301504 | bytes 9437248 | tf_op jit(solution)/shard_map/cb,kbt->kct/dot_general | solution.py:37
  138.8 0.4 reshape.20
  139.3 0.7 convolution_convert_fusion.1
  140.0 1.0 all_to_all.23
  141.0 6.7 %all-to-all-start.1 = ((bf16[8,32,1024]{2,1,0:T(8,128)(2,1)}), bf16[8,32,1024]{2,1,0:T(8,128)(2,1)S(1)}, u32[]{:S(2)}, u32[]{:S(2)}) async-start(bf16[8,32,1024]{2,1,0:T(8,128)(2,1)} %all_to_all.23), calls=%async_computation.1 | async-start | bytes 1048576 | tf_op jit(solution)/shard_map/all_to_all | solution.py:30
  147.7 29.3 %all-to-all-done.1 = bf16[8,32,1024]{2,1,0:T(8,128)(2,1)S(1)} async-done(((bf16[8,32,1024]{2,1,0:T(8,128)(2,1)}), bf16[8,32,1024]{2,1,0:T(8,128)(2,1)S(1)}, u32[]{:S(2)}, u32[]{:S(2)}) %all-to-all-start.1) | async-done | bytes 524320 | tf_op jit(solution)/shard_map/all_to_all | solution.py:30
  177.0 1.2 gather_fusion
  178.2 0.1 broadcast_select_fusion.4
  178.4 1.9 collective-permute-done
  180.3 1.2 gather_fusion.1
  181.5 0.1 broadcast_select_fusion.3
  181.6 67.0 %all-gather.2.cloned.1.call-done = bf16[4,2048,1024]{2,1,0:T(8,128)(2,1)} async-done(((bf16[4,256,1024]{2,1,0:T(8,128)(2,1)}), bf16[4,2048,1024]{2,1,0:T(8,128)(2,1)}) %all-gather.2.cloned.1.call-update) | async-done | bytes 16777232 | tf_op jit(solution)/shard_map/all_gather | solution.py:51
  248.6 3.4 %fusion.5 = bf16[256,1024]{1,0:T(8,128)(2,1)S(1)} fusion(bf16[4,2048,1024]{2,1,0:T(8,128)(2,1)} %all-gather.2.cloned.1.call-done, bf16[256,1024]{1,0:T(8,128)(2,1)S(1)} %broadcast_select_fusion.3, bf16[256,1024]{1,0:T(8,128)(2,1)S(1)} %broadcast_select_fusion.4), kind=kOutput, calls=%fused_computation.16 | convolution fusion | flops 1076101120 | bytes 5767168 | tf_op jit(solution)/shard_map/dot_general | solution.py:57
  252.1 1.5 collective-permute-start.1
  253.6 12.0 %collective-permute-done.1 = bf16[256,1024]{1,0:T(8,128)(2,1)S(1)} collective-permute-done((bf16[256,1024]{1,0:T(8,128)(2,1)S(1)}, bf16[256,1024]{1,0:T(8,128)(2,1)S(1)}, u32[]{:S(2)}, u32[]{:S(2)}) %collective-permute-start.1) | collective-permute-done | bytes 524320 | tf_op jit(solution)/shard_map/ppermute | solution.py:16
  265.6 1.2 gather_fusion.2
  266.8 0.1 broadcast_select_fusion.2
  266.9 3.5 %fusion.6 = bf16[256,1024]{1,0:T(8,128)(2,1)S(1)} fusion(bf16[4,2048,1024]{2,1,0:T(8,128)(2,1)} %all-gather.2.cloned.1.call-done, bf16[256,1024]{1,0:T(8,128)(2,1)S(1)} %broadcast_select_fusion.2, bf16[256,1024]{1,0:T(8,128)(2,1)S(1)} %fusion.5), kind=kOutput, calls=%fused_computation.17 | convolution fusion | flops 1076101120 | bytes 5767168 | tf_op jit(solution)/shard_map/dot_general | solution.py:57
  270.5 12.6 %collective-permute-done.2 = bf16[256,1024]{1,0:T(8,128)(2,1)S(1)} collective-permute-done((bf16[256,1024]{1,0:T(8,128)(2,1)S(1)}, bf16[256,1024]{1,0:T(8,128)(2,1)S(1)}, u32[]{:S(2)}, u32[]{:S(2)}) %collective-permute-start.2) | collective-permute-done | bytes 524320 | tf_op jit(solution)/shard_map/ppermute | solution.py:16
  283.1 1.2 gather_fusion.3
  284.3 0.1 broadcast_select_fusion.1
  284.4 3.5 %fusion.7 = bf16[256,1024]{1,0:T(8,128)(2,1)S(1)} fusion(bf16[4,2048,1024]{2,1,0:T(8,128)(2,1)} %all-gather.2.cloned.1.call-done, bf16[256,1024]{1,0:T(8,128)(2,1)S(1)} %broadcast_select_fusion.1, bf16[256,1024]{1,0:T(8,128)(2,1)S(1)} %fusion.6), kind=kOutput, calls=%fused_computation.18 | convolution fusion | flops 1076101120 | bytes 5767168 | tf_op jit(solution)/shard_map/dot_general | solution.py:57
  287.9 0.7 collective-permute-start.3
  288.6 23.3 %collective-permute-done.3 = bf16[256,1024]{1,0:T(8,128)(2,1)S(1)} collective-permute-done((bf16[256,1024]{1,0:T(8,128)(2,1)S(1)}, bf16[256,1024]{1,0:T(8,128)(2,1)S(1)}, u32[]{:S(2)}, u32[]{:S(2)}) %collective-permute-start.3) | collective-permute-done | bytes 524320 | tf_op jit(solution)/shard_map/ppermute | solution.py:16
  311.8 1.2 gather_fusion.4
  313.1 4.2 %fusion.8 = bf16[256,1024]{1,0:T(8,128)(2,1)} fusion(bf16[4,2048,1024]{2,1,0:T(8,128)(2,1)} %all-gather.2.cloned.1.call-done, bf16[256,1024]{1,0:T(8,128)(2,1)S(1)} %broadcast_select_fusion, bf16[256,1024]{1,0:T(8,128)(2,1)S(1)} %fusion.7), kind=kOutput, calls=%fused_computation.19 | convolution fusion | flops 1076101120 | bytes 5767168 | tf_op jit(solution)/shard_map/dot_general | solution.py:57
  (27 shorter events, 0.4 us)
Async XLA Ops:
  6.5 126.7 %copy-start = (bf16[2,16]{1,0:T(2,128)(2,1)S(1)}, bf16[2,16]{1,0:T(2,128)(2,1)}, u32[]{:S(2)}) copy-start(bf16[2,16]{1,0:T(2,128)(2,1)} %param.8) | copy-start | bytes 196
  6.5 242.1 %all-gather.2.cloned.1.call-start = ((), (), s32[]{:S(2)}) async-start(), calls=%async_computation.2 | async-start | bytes 18874368 | tf_op jit(solution)/shard_map/all_gather | solution.py:51
  7.3 99.5 %all-to-all-start = ((bf16[4,4096,256]{2,1,0:T(8,128)(2,1)}), bf16[4,4096,256]{2,1,0:T(8,128)(2,1)}, u32[]{:S(2)}, u32[]{:S(2)}) async-start(bf16[4,4096,256]{2,1,0:T(8,128)(2,1)} %bitcast.35), calls=%async_computation | async-start | bytes 16777216 | tf_op jit(solution)/shard_map/all_to_all | solution.py:34
  139.3 8.4 %copy-start.2 = (s32[256]{0:T(256)S(1)}, s32[256]{0:T(256)}, u32[]{:S(2)}) copy-start(s32[256]{0:T(256)} %param.10) | copy-start | bytes 3076
  139.3 8.4 %copy-start.1 = (s32[4,256]{1,0:T(4,128)S(1)}, s32[4,256]{1,0:T(4,128)}, u32[]{:S(2)}) copy-start(s32[4,256]{1,0:T(4,128)} %param.11) | copy-start | bytes 12292
  141.0 36.0 %all-to-all-start.1 = ((bf16[8,32,1024]{2,1,0:T(8,128)(2,1)}), bf16[8,32,1024]{2,1,0:T(8,128)(2,1)S(1)}, u32[]{:S(2)}, u32[]{:S(2)}) async-start(bf16[8,32,1024]{2,1,0:T(8,128)(2,1)} %all_to_all.23), calls=%async_computation.1 | async-start | bytes 1048576 | tf_op jit(solution)/shard_map/all_to_all | solution.py:30
  178.3 2.0 collective-permute-start
  252.1 13.6 %collective-permute-start.1 = (bf16[256,1024]{1,0:T(8,128)(2,1)S(1)}, bf16[256,1024]{1,0:T(8,128)(2,1)S(1)}, u32[]{:S(2)}, u32[]{:S(2)}) collective-permute-start(bf16[256,1024]{1,0:T(8,128)(2,1)S(1)} %fusion.5), channel_id=1, source_target_pairs={{0,2},{1,3},{2,0},{3,1},{4,6},{5,7},{6,4},{7,5},{8,10},{9,11},{10,... | collective-permute-start | bytes 1572872 | tf_op jit(solution)/shard_map/ppermute | solution.py:16
  270.4 12.7 %collective-permute-start.2 = (bf16[256,1024]{1,0:T(8,128)(2,1)S(1)}, bf16[256,1024]{1,0:T(8,128)(2,1)S(1)}, u32[]{:S(2)}, u32[]{:S(2)}) collective-permute-start(bf16[256,1024]{1,0:T(8,128)(2,1)S(1)} %fusion.6), channel_id=1, source_target_pairs={{0,4},{1,5},{2,6},{3,7},{4,0},{5,1},{6,2},{7,3},{8,12},{9,13},{10,... | collective-permute-start | bytes 1572872 | tf_op jit(solution)/shard_map/ppermute | solution.py:16
  287.9 24.0 %collective-permute-start.3 = (bf16[256,1024]{1,0:T(8,128)(2,1)S(1)}, bf16[256,1024]{1,0:T(8,128)(2,1)S(1)}, u32[]{:S(2)}, u32[]{:S(2)}) collective-permute-start(bf16[256,1024]{1,0:T(8,128)(2,1)S(1)} %fusion.7), channel_id=1, source_target_pairs={{0,8},{1,9},{2,10},{3,11},{4,12},{5,13},{6,14},{7,15},{8,0},{9,1},... | collective-permute-start | bytes 1572872 | tf_op jit(solution)/shard_map/ppermute | solution.py:16
Sparse Core Ops, SparseCore 0:
  9.5 239.1 all-gather.1
where the time goes:
time: 325 us; the launch traced here: 324 us
  waiting for transfers between devices  236 us (73%)
  local copies, waits for them, and re-layouts  33.8 us (10%)
  matrix products  20.9 us (6%)
  starting transfers between devices  14.7 us (5%)
  between operations  13.6 us (4%)
  other arithmetic  5.44 us (2%)
    all_to_all x1, waiting for transfers between devices, on_device(): lax.all_to_all(traces, 'ta', split_axis=0, concat_axis=1, tiled=True)  89 us
    all_gather x1, waiting for transfers between devices, on_device(): every_level = lax.all_gather(translations, ('gx', 'gy'), axis=1, tiled=True)  67 us
    ppermute x4, waiting for transfers between devices, from_partner(): return lax.ppermute(value, axis, pairs)  49.7 us
    all_to_all x1, waiting for transfers between devices, move_boxes(): lax.all_to_all(blocks, ('gx', 'gy'), split_axis=0, concat_axis=0, tiled=T...  29.3 us
    dot_general x4, matrix products, on_device(): jnp.dot(joined, every_level[layer_index], preferred_element_type=jnp.floa...  14.6 us
    reshape x1, local copies, waits for them, and re-layouts, on_device(): regrouped.reshape(box_count, BOXT, sample_count)  14.4 us
    all_to_all x1, local copies, waits for them, and re-layouts, on_device(): lax.all_to_all(traces, 'ta', split_axis=0, concat_axis=1, tiled=True)  12.2 us
    all_to_all x1, starting transfers between devices, move_boxes(): lax.all_to_all(blocks, ('gx', 'gy'), split_axis=0, concat_axis=0, tiled=T...  6.66 us
  transfers between devices with their start and end apart: 7, of which 7 were waited for; matrix products, arithmetic and copies ran while one was open for 13% of the time, Pallas kernels for 0%

commit v1 on v0

v1 whole, which is shorter than its diff:
```python
import functools
import math

import jax
import jax.numpy as jnp
import numpy as np
from jax import lax
from jax.experimental import pallas as pl
from jax.experimental.pallas import tpu as pltpu
from jax.sharding import PartitionSpec as P

NF = 256
CHEB = 2
BOXT = 16
BLOCK_BOXES = 16
TILE = 256
MESH = pl.DeviceIdType.MESH


def spectrum_table(length, count):
    sample_pos = np.arange(length, dtype=np.float32)[:, None]
    frequency = np.arange(count, dtype=np.float32)[None, :] + np.float32(1.0)
    angles = np.float32(2.0 * math.pi / length) * np.mod(sample_pos * frequency, np.float32(length))
    factor = np.float32(math.sqrt(2.0 / length))
    table = np.concatenate([np.cos(angles) * factor, -np.sin(angles) * factor], axis=1)
    return table.astype(jnp.bfloat16)


def flip(index, mask, size):
    result = index
    bit = 1
    while bit < size:
        if mask & bit:
            result = result + bit - 2 * bit * ((index // bit) % 2)
        bit *= 2
    return result


def kernel(
    sizes,
    traces,
    interp,
    translations,
    slots,
    pairs,
    table,
    out,
    tr,
    weights,
    mat,
    sampled,
    slices,
    fourier,
    acc,
    points,
    arrived,
    states,
    partner,
    select,
    load_sem,
    table_sem,
    own_sem,
    ag_send,
    ag_recv,
    core_send,
    core_recv,
    ta_send,
    ta_recv,
    g_send,
    g_recv,
    level_send,
    level_recv,
):
    n_gx, n_gy, n_ta = sizes
    groups = n_gx * n_gy
    gx, gy, ta = lax.axis_index("gx"), lax.axis_index("gy"), lax.axis_index("ta")
    group = gx * n_gy + gy
    level_count = translations.shape[0]
    rows = translations.shape[1]
    half = rows // 2
    width = translations.shape[2]
    boxes = slots.shape[1]
    span = traces.shape[1]
    block = boxes * BOXT
    chunk = states.shape[3]
    chunks = width // chunk
    log_devices = (groups * n_ta).bit_length() - 1
    side = ta % 2

    def of_group(offset):
        p = flip(group, offset, groups)
        return (p // n_gy, p % n_gy, ta)

    def of_ta(offset):
        return (gx, gy, flip(ta, offset, n_ta))

    def loading(j):
        t = flip(ta, j, n_ta)
        return pltpu.make_async_copy(
            traces.at[pl.ds(pl.multiple_of(t * block, block), block), :], tr.at[j], load_sem.at[j]
        )

    def own(level):
        return [
            pltpu.make_async_copy(
                translations.at[level, pl.ds(part * half, half), :],
                weights.at[level, group, part],
                own_sem.at[level, part],
            )
            for part in range(2)
        ]

    bits = []
    bit = n_gy // 2
    while bit:
        bits.append(bit)
        bit //= 2
    bit = n_gx // 2
    while bit:
        bits.append(bit * n_gy)
        bit //= 2
    stage_of = {0: -1}
    order = [0]
    for stage, bit in enumerate(bits):
        for offset in list(order):
            stage_of[offset ^ bit] = stage
            order.append(offset ^ bit)

    def shard(level, offset):
        return weights.at[level, flip(group, offset, groups), side]

    def passing(level, offset, stage):
        bit = bits[stage]
        return pltpu.make_async_remote_copy(
            src_ref=shard(level, offset),
            dst_ref=shard(level, offset),
            send_sem=ag_send.at[level, offset ^ bit],
            recv_sem=ag_recv.at[level, offset ^ bit],
            device_id=of_group(bit),
            device_id_type=MESH,
        )

    def landed(level, offset):
        bit = bits[stage_of[offset]]
        return pltpu.make_async_remote_copy(
            src_ref=shard(level, offset),
            dst_ref=shard(level, offset),
            send_sem=ag_send.at[level, offset],
            recv_sem=ag_recv.at[level, offset],
            device_id=of_group(bit),
            device_id_type=MESH,
        )

    def sharing(level, offset, mine):
        place = weights.at[
            level, flip(group, offset, groups), side if mine else flip(side, 1, 2)
        ]
        return pltpu.make_async_remote_copy(
            src_ref=place,
            dst_ref=place,
            send_sem=core_send.at[level, offset],
            recv_sem=core_recv.at[level, offset],
            device_id=of_ta(1),
            device_id_type=MESH,
        )

    def pump(level, stage):
        if stage == 0:
            for copy in own(level):
                copy.wait()
        for offset in order:
            if stage_of[offset] != stage - 1:
                continue
            if offset:
                landed(level, offset).wait_recv()
                sharing(level, offset, True).start()
            for later in range(stage, len(bits)):
                passing(level, offset, later).start()

    stages = len(bits)

    reached = [0]

    def pumps(step):
        while reached[0] <= step:
            for level in range(level_count):
                stage = reached[0] - level
                if 0 <= stage <= stages:
                    pump(level, stage)
            reached[0] += 1

    def finish(level):
        for offset in order[1:]:
            sharing(level, offset, False).wait_recv()

    def regroup(j):
        return pltpu.make_async_remote_copy(
            src_ref=sampled.at[j],
            dst_ref=slices.at[j],
            send_sem=ta_send.at[j],
            recv_sem=ta_recv.at[j],
            device_id=of_ta(j),
            device_id_type=MESH,
        )

    def moving(offset, sending):
        src = points.at[flip(group, offset, groups)]
        dst = arrived.at[group if sending else flip(group, offset, groups)]
        return pltpu.make_async_remote_copy(
            src_ref=src,
            dst_ref=dst,
            send_sem=g_send.at[offset],
            recv_sem=g_recv.at[offset],
            device_id=of_group(offset),
            device_id_type=MESH,
        )

    def exchange(level, k):
        mask = 2 ** (level * log_devices // level_count)
        target = of_ta(mask) if mask < n_ta else of_group(mask // n_ta)
        return pltpu.make_async_remote_copy(
            src_ref=states.at[level, k],
            dst_ref=partner.at[level, k],
            send_sem=level_send.at[level, k],
            recv_sem=level_recv.at[level, k],
            device_id=target,
            device_id_type=MESH,
        )

    near = [n_ta - 1 - j for j in range(n_ta)]
    for j in near:
        loading(j).start()
    for level in range(level_count):
        for copy in own(level):
            copy.start()
    table_copy = pltpu.make_async_copy(table, fourier, table_sem)
    table_copy.start()

    barrier = pltpu.get_barrier_semaphore()
    for j in range(1, n_ta):
        pl.semaphore_signal(barrier, inc=1, device_id=of_ta(j), device_id_type=MESH)
    for offset in range(1, groups):
        pl.semaphore_signal(barrier, inc=1, device_id=of_group(offset), device_id_type=MESH)

    columns = BLOCK_BOXES * BOXT
    spread = (
        lax.broadcasted_iota(jnp.int32, (BOXT, columns), 1) % BOXT
        == lax.broadcasted_iota(jnp.int32, (BOXT, columns), 0)
    )
    tiled = jnp.dot(
        interp[...], spread.astype(jnp.float32).astype(jnp.bfloat16), preferred_element_type=jnp.float32
    )
    own_box = (
        lax.broadcasted_iota(jnp.int32, (BLOCK_BOXES, columns), 1) // BOXT
        == lax.broadcasted_iota(jnp.int32, (BLOCK_BOXES, columns), 0)
    )
    for c in range(CHEB):
        mat[pl.ds(c * BLOCK_BOXES, BLOCK_BOXES), :] = jnp.where(
            own_box, tiled[c : c + 1, :], 0.0
        ).astype(jnp.bfloat16)

    def selection(index_row):
        hit = lax.broadcasted_iota(jnp.int32, (boxes, boxes), 0) == index_row
        return jnp.where(hit, 1.0, 0.0).T.astype(jnp.bfloat16)

    select[0] = selection(slots[...])
    for level in range(level_count):
        select[level + 1] = selection(pairs[pl.ds(level, 1), :])

    pl.semaphore_wait(barrier, n_ta - 1 + groups - 1)
    pumps(0)

    for j in near:
        loading(j).wait()
        where = sampled if j else slices

        def interpolate(i, carry):
            traces_block = tr[j, pl.ds(pl.multiple_of(i * columns, columns), columns), :]
            both = jnp.dot(mat[...], traces_block, preferred_element_type=jnp.float32)
            both = both.astype(jnp.bfloat16)
            place = pl.ds(pl.multiple_of(i * BLOCK_BOXES, BLOCK_BOXES), BLOCK_BOXES)
            for c in range(CHEB):
                where[j, c, place, :] = both[c * BLOCK_BOXES : (c + 1) * BLOCK_BOXES, :]
            return carry

        lax.fori_loop(0, boxes // BLOCK_BOXES, interpolate, 0, unroll=4)
        if j:
            regroup(j).start()

    pumps(1)
    table_copy.wait()
    for j in range(n_ta):
        if j:
            regroup(j).wait_recv()
        first = pl.multiple_of(flip(ta, j, n_ta) * span, span)
        for c in range(CHEB):
            part = jnp.dot(
                slices[j, c], fourier[pl.ds(first, span), :], preferred_element_type=jnp.float32
            )
            cols = pl.ds(c * 2 * NF, 2 * NF)
            if j:
                acc[:, cols] += part
            else:
                acc[:, cols] = part
    points[...] = acc[...].reshape(points.shape).astype(jnp.bfloat16)
    for offset in range(groups - 1, 0, -1):
        moving(offset, True).start()
    arrived[group] = points[group]
    pumps(2)
    for offset in range(1, groups):
        moving(offset, False).wait_recv()

    for k in range(chunks):
        boxes_in = arrived[:, :, k * chunk : (k + 1) * chunk].astype(jnp.float32)
        boxes_in = boxes_in.reshape(boxes, chunk).astype(jnp.bfloat16)
        states[0, k] = jnp.dot(select[0], boxes_in, preferred_element_type=jnp.float32).astype(
            jnp.bfloat16
        )
        exchange(0, k).start()

    per_chunk = chunk // rows

    def weight(level, k, cols):
        piece = weights[level, k * per_chunk : (k + 1) * per_chunk, :, :, cols]
        return piece.reshape(chunk, chunk)

    for level in range(level_count):
        pumps(level + stages)
        finish(level)

        def own_part(n, carry):
            cols = pl.ds(pl.multiple_of(n * chunk, chunk), chunk)
            total = jnp.zeros((boxes, chunk), jnp.float32)
            for k in range(chunks):
                total += jnp.dot(
                    states[level, k], weight(level, k, cols), preferred_element_type=jnp.float32
                )
            acc[:, cols] = total
            return carry

        lax.fori_loop(0, chunks, own_part, 0)
        for k in range(chunks):
            exchange(level, k).wait_recv()
            aligned = jnp.dot(
                select[level + 1], partner[level, k], preferred_element_type=jnp.float32
            ).astype(jnp.bfloat16)
            if k < chunks - 1:

                def partner_part(n, carry):
                    cols = pl.ds(pl.multiple_of(n * chunk, chunk), chunk)
                    acc[:, cols] += jnp.dot(
                        aligned, weight(level, chunks + k, cols), preferred_element_type=jnp.float32
                    )
                    return carry

                lax.fori_loop(0, chunks, partner_part, 0)
            else:
                for n in range(chunks):
                    cols = pl.ds(n * chunk, chunk)
                    total = acc[:, cols] + jnp.dot(
                        aligned, weight(level, chunks + k, cols), preferred_element_type=jnp.float32
                    )
                    if level < level_count - 1:
                        states[level + 1, n] = total.astype(jnp.bfloat16)
                        exchange(level + 1, n).start()
                    else:
                        out[:, cols] = total.astype(jnp.bfloat16)

    for j in range(1, n_ta):
        regroup(j).wait_send()
    for offset in range(1, groups):
        moving(offset, True).wait_send()
    for level in range(level_count):
        for k in range(chunks):
            exchange(level, k).wait_send()
        for offset in order[1:]:
            landed(level, offset).wait_send()
            sharing(level, offset, True).wait_send()


def on_device(sizes, traces, interp, translations, leaf_slot, pairing):
    n_gx, n_gy, n_ta = sizes
    groups = n_gx * n_gy
    boxes = leaf_slot.shape[0]
    levels, rows, width = translations.shape
    span = traces.shape[1]
    block = traces.shape[0] // n_ta
    chunk = max(TILE, rows)
    chunks = width // chunk
    table = jnp.asarray(spectrum_table(span * n_ta, NF))
    bf16, f32 = jnp.bfloat16, jnp.float32
    anywhere = pl.BlockSpec(memory_space=pl.ANY)
    vmem = pl.BlockSpec(memory_space=pltpu.VMEM)
    dma = pltpu.SemaphoreType.DMA
    return pl.pallas_call(
        functools.partial(kernel, sizes),
        out_shape=jax.ShapeDtypeStruct((boxes, width), bf16),
        in_specs=[anywhere, vmem, anywhere, vmem, vmem, anywhere],
        out_specs=vmem,
        scratch_shapes=[
            pltpu.VMEM((n_ta, block, span), bf16),
            pltpu.VMEM((levels, groups, 2, rows // 2, width), bf16),
            pltpu.VMEM((CHEB * BLOCK_BOXES, BLOCK_BOXES * BOXT), bf16),
            pltpu.VMEM((n_ta, CHEB, boxes, span), bf16),
            pltpu.VMEM((n_ta, CHEB, boxes, span), bf16),
            pltpu.VMEM(table.shape, bf16),
            pltpu.VMEM((boxes, width), f32),
            pltpu.VMEM((groups, boxes // groups, width), bf16),
            pltpu.VMEM((groups, boxes // groups, width), bf16),
            pltpu.VMEM((levels, chunks, boxes, chunk), bf16),
            pltpu.VMEM((levels, chunks, boxes, chunk), bf16),
            pltpu.VMEM((levels + 1, boxes, boxes), bf16),
            dma((n_ta,)),
            dma,
            dma((levels, 2)),
            dma((levels, groups)),
            dma((levels, groups)),
            dma((levels, groups)),
            dma((levels, groups)),
            dma((n_ta,)),
            dma((n_ta,)),
            dma((groups,)),
            dma((groups,)),
            dma((levels, chunks)),
            dma((levels, chunks)),
        ],
        compiler_params=pltpu.CompilerParams(
            collective_id=0, has_side_effects=True, vmem_limit_bytes=60 * 2**20
        ),
    )(traces, interp, translations, leaf_slot.reshape(1, boxes), pairing, table)


def solution(mesh):
    sizes = (mesh.shape["gx"], mesh.shape["gy"], mesh.shape["ta"])
    in_specs = (
        P(("gx", "gy"), "ta"),
        P(),
        P(None, ("gx", "gy"), None),
        P(("gx", "gy", "ta")),
        P(None, ("gx", "gy", "ta")),
    )
    out_specs = P(("gx", "gy", "ta"), None)
    return jax.shard_map(
        functools.partial(on_device, sizes),
        mesh=mesh,
        in_specs=in_specs,
        out_specs=out_specs,
        check_vma=False,
    )
```

time: 325 us -> 127 us (0.39)
  waiting for transfers between devices: 236 us -> 0 us
  Pallas kernels: 0 us -> 124 us
  local copies, waits for them, and re-layouts: 33.8 us -> 1.87 us
  matrix products: 20.9 us -> 0 us
  starting transfers between devices: 14.7 us -> 0 us
  between operations: 13.6 us -> 0.01 us
  other arithmetic: 5.44 us -> 0 us
    pallas_call x0 -> x1, Pallas kernels: none -> 124 us  [on_device(): pl.pallas_call(functools.partial(kernel, sizes), out_shape=jax.ShapeDtype...]
    all_to_all x2 -> x0, waiting for transfers between devices: 118 us -> none  [the longest x1 89 us: on_device(): lax.all_to_all(traces, 'ta', split_axis=0, concat_axis=1, tiled=True)]
    all_gather x1 -> x0, waiting for transfers between devices: 67 us -> none  [on_device(): every_level = lax.all_gather(translations, ('gx', 'gy'), axis=1, tiled=True)]
    ppermute x4 -> x0, waiting for transfers between devices: 49.7 us -> none  [from_partner(): return lax.ppermute(value, axis, pairs)]
    dot_general x6 -> x0, matrix products: 20.9 us -> none  [the longest x4 14.6 us: on_device(): jnp.dot(joined, every_level[layer_index], preferred_element_type=jnp.floa...]
    reshape x2 -> x0, local copies, waits for them, and re-layouts: 14.8 us -> none  [the longest x1 14.4 us: on_device(): regrouped.reshape(box_count, BOXT, sample_count)]
    all_to_all x2 -> x0, local copies, waits for them, and re-layouts: 13.1 us -> none  [the longest x1 12.2 us: on_device(): lax.all_to_all(traces, 'ta', split_axis=0, concat_axis=1, tiled=True)]
    all_to_all x2 -> x0, starting transfers between devices: 12.3 us -> none  [the longest x1 6.66 us: move_boxes(): lax.all_to_all(blocks, ('gx', 'gy'), split_axis=0, concat_axis=0, tiled=T...]
  transfers between devices with their start and end apart: 7 -> 0, of which waited for: 7 -> 0; matrix products, arithmetic and copies ran while one was open for 13% -> 0% of each run, Pallas kernels for 0% -> 0%
where the time goes in v1:
time: 127 us; the launch traced here: 126 us
  Pallas kernels  124 us (98%)
  local copies, waits for them, and re-layouts  1.87 us (1%)
    pallas_call x1, Pallas kernels, on_device(): pl.pallas_call(functools.partial(kernel, sizes), out_shape=jax.ShapeDtype...  124 us

profile of v1, /device:TPU:0, one launch (start us, length us, event | category | flops | bytes accessed | tf_op | source)
XLA Modules:
  0.0 126.4 jit_solution(156943696915368910)
XLA Ops:
  0.0 124.5 %shard_map.64 = bf16[256,1024]{1,0:T(8,128)(2,1)} custom-call(bf16[16384,256]{1,0:T(8,128)(2,1)} %traces.1, bf16[2,16]{1,0:T(2,128)(2,1)} %interp.1, bf16[4,256,1024]{2,1,0:T(8,128)(2,1)} %translations.1, s32[1,256]{1,0:T(1,128)} %bitcast.1, s32[4,256]{1,0:T(4,128)} %pairs.1, bf16[1024,512]{1,0:T(8,128)(2,1)} %constant.2.clone.table), custom_call_target="tpu_custom_call" | custom-call | tf_op jit(solution)/shard_map/pallas_call | solution.py:395
  124.5 1.9 %copy.8 = bf16[256,1024]{1,0:T(8,128)(2,1)} copy(bf16[256,1024]{1,0:T(8,128)(2,1)} %shard_map.64) | data formatting | bytes 1048576
